TPU v7x, 32 devices: a whole 2x2x4 slice. The times are simulated.
32 devices in a mesh: uly: 2 (over y), blk: 16 (over z, x, core).
Axes of the slice: x: 2, y: 2, z: 4, core: 2. Of those that a mesh axis runs over, the one named last changes fastest.
Arguments:
- query_inputs: bfloat16 [4096, 2048], P(('blk', 'uly')), may hold values from -6 to 6
- key_inputs: bfloat16 [4096, 1024], P(('blk', 'uly')), may hold values from -6 to 6
- value_inputs: bfloat16 [4096, 1024], P(('blk', 'uly')), may hold values from -6 to 6
- forward_out: bfloat16 [4096, 2048], P(('blk', 'uly')), may hold values from -6 to 6
- output_gradient: bfloat16 [4096, 2048], P(('blk', 'uly')), may hold values from -4 to 4
- lse_parts: float32 [4096, 16, 2], P(('blk', 'uly')), may hold values from 3 to 247
- segment_ids: int32 [4096], P(('blk', 'uly')), may hold values from 0 to 31, never falling along the last dimension, each value on 1 to 512 neighbouring positions
Outputs:
- query_grad: bfloat16 [4096, 2048], P(('blk', 'uly'))
- key_grad: bfloat16 [4096, 1024], P(('blk', 'uly'))
- value_grad: bfloat16 [4096, 1024], P(('blk', 'uly'))
Inputs may be any that keep to these rules, and one draw needn't show every extreme that they name: `segment_ids`: never falls along the sequence; every document holds 1 to 512 tokens, and some document exactly 512.
All inputs are finite; a program needn't handle non-finite values.
Results may differ from a plain program's by a relative error of at most 0.0051.
Values may be sent and summed in bfloat16 or wider, within the bound.
A program may use at most 128 MiB of HBM per device.

v0:
```python
import math
import jax
import jax.numpy as jnp
from jax import lax
from jax.sharding import PartitionSpec as P

HEAD_SIZE = 128
QUERY_HEADS = 16
KEY_VALUE_HEADS = 8
HOPS = 2
QBLOCK = 512


def from_behind(block, axis, distance):
    devices = range(lax.axis_size(axis))
    route = [(i - distance, i) for i in devices if i - distance in devices]
    return lax.ppermute(block, axis, route)


def merge_parts(partials):
    highest = jnp.max(partials, axis=-1)
    return highest + jnp.log(jnp.sum(jnp.exp(partials - highest[..., None]), axis=-1))


def row_delta(grad_rows, out_rows):
    row_total = grad_rows.shape[0]
    products = grad_rows.astype(jnp.float32) * out_rows.astype(jnp.float32)
    return jnp.sum(products.reshape(row_total, -1, HEAD_SIZE), axis=-1)


def tile_grads(query_blk, grad_blk, lse_blk, delta_blk, key_blk, value_blk, allowed):
    score_scale = 1.0 / math.sqrt(HEAD_SIZE)
    scores = (
        jnp.einsum("mhgd,nhd->hgmn", query_blk, key_blk, preferred_element_type=jnp.float32)
        * score_scale
    )
    weights = jnp.where(allowed, jnp.exp(scores - lse_blk), 0.0)
    value_portion = jnp.einsum(
        "hgmn,mhgd->nhd", weights.astype(jnp.bfloat16), grad_blk, preferred_element_type=jnp.float32
    )
    prob_grad = jnp.einsum(
        "mhgd,nhd->hgmn", grad_blk, value_blk, preferred_element_type=jnp.float32
    )
    score_grad = (weights * (prob_grad - delta_blk)).astype(jnp.bfloat16)
    query_part = (
        jnp.einsum("hgmn,nhd->mhgd", score_grad, key_blk, preferred_element_type=jnp.float32)
        * score_scale
    )
    key_portion = (
        jnp.einsum("hgmn,mhgd->nhd", score_grad, query_blk, preferred_element_type=jnp.float32)
        * score_scale
    )
    return (query_part, key_portion, value_portion)


def per_device(
    query_inputs, key_inputs, value_inputs, forward_out, output_gradient, lse_parts, segment_ids
):
    uly_count = lax.axis_size("uly")
    blk_place = lax.axis_index("blk")
    tok_local = query_inputs.shape[0]
    row_count = tok_local * uly_count
    group_width = QUERY_HEADS // KEY_VALUE_HEADS
    query_loc, grad_loc, key_loc, value_loc, out_loc = (
        lax.all_to_all(query_inputs, "uly", split_axis=1, concat_axis=0, tiled=True),
        lax.all_to_all(output_gradient, "uly", split_axis=1, concat_axis=0, tiled=True),
        lax.all_to_all(key_inputs, "uly", split_axis=1, concat_axis=0, tiled=True),
        lax.all_to_all(value_inputs, "uly", split_axis=1, concat_axis=0, tiled=True),
        lax.all_to_all(forward_out, "uly", split_axis=1, concat_axis=0, tiled=True),
    )
    parts_loc = lax.all_to_all(
        lse_parts.reshape(tok_local, -1), "uly", split_axis=1, concat_axis=0, tiled=True
    )
    lse_loc = merge_parts(parts_loc.reshape(row_count, -1, 2))
    delta_loc = row_delta(grad_loc, out_loc)
    ids_loc = lax.all_gather(segment_ids, "uly", axis=0, tiled=True)
    kv_heads = key_loc.shape[1] // HEAD_SIZE
    query_quad = query_loc.reshape(row_count, kv_heads, group_width, HEAD_SIZE)
    gradient_quad = grad_loc.reshape(row_count, kv_heads, group_width, HEAD_SIZE)
    logsumexp_cube = lse_loc.reshape(row_count, kv_heads, group_width).transpose(1, 2, 0)[..., None]
    delta_cube = delta_loc.reshape(row_count, kv_heads, group_width).transpose(1, 2, 0)[..., None]
    key_cube = key_loc.reshape(row_count, kv_heads, HEAD_SIZE)
    value_cube = value_loc.reshape(row_count, kv_heads, HEAD_SIZE)
    rows_per_block = min(QBLOCK, row_count)
    block_total = row_count // rows_per_block
    position = jnp.arange(row_count, dtype=jnp.int32)
    query_parts = []
    key_gradient_running = jnp.zeros((row_count, kv_heads, HEAD_SIZE), jnp.float32)
    value_gradient_running = jnp.zeros((row_count, kv_heads, HEAD_SIZE), jnp.float32)
    for block_index in range(block_total):
        leading_row = block_index * rows_per_block
        finish = leading_row + rows_per_block
        allowed = (position[None, :finish] <= position[leading_row:finish, None]) & (
            ids_loc[None, :finish] == ids_loc[leading_row:finish, None]
        )
        tile_out = tile_grads(
            query_quad[leading_row:finish],
            gradient_quad[leading_row:finish],
            logsumexp_cube[:, :, leading_row:finish],
            delta_cube[:, :, leading_row:finish],
            key_cube[:finish],
            value_cube[:finish],
            allowed,
        )
        query_parts.append(tile_out[0])
        padding = ((0, row_count - finish), (0, 0), (0, 0))
        key_gradient_running = key_gradient_running + jnp.pad(tile_out[1], padding)
        value_gradient_running = value_gradient_running + jnp.pad(tile_out[2], padding)
    query_acc = jnp.concatenate(query_parts, axis=0)
    stacked_kv = jnp.stack([key_loc, value_loc])
    moved_kv = stacked_kv
    moved_ids = ids_loc
    key_parts = []
    for hop_index in range(1, HOPS + 1):
        moved_kv = from_behind(stacked_kv, "blk", hop_index)
        moved_ids = from_behind(ids_loc, "blk", hop_index)
        live = (blk_place >= hop_index) & (moved_ids[-1] == ids_loc[0])
        moved_key = moved_kv[0].reshape(row_count, kv_heads, HEAD_SIZE)
        moved_value = moved_kv[1].reshape(row_count, kv_heads, HEAD_SIZE)

        def compute_tile(unused):
            query_pieces = []
            key_sum = jnp.zeros((row_count, kv_heads, HEAD_SIZE), jnp.float32)
            value_sum = jnp.zeros((row_count, kv_heads, HEAD_SIZE), jnp.float32)
            for block_index in range(block_total):
                leading_row = block_index * rows_per_block
                finish = leading_row + rows_per_block
                allowed = moved_ids[None, :] == ids_loc[leading_row:finish, None]
                tile_out = tile_grads(
                    query_quad[leading_row:finish],
                    gradient_quad[leading_row:finish],
                    logsumexp_cube[:, :, leading_row:finish],
                    delta_cube[:, :, leading_row:finish],
                    moved_key,
                    moved_value,
                    allowed,
                )
                query_pieces.append(tile_out[0])
                key_sum = key_sum + tile_out[1]
                value_sum = value_sum + tile_out[2]
            stacked = jnp.stack([key_sum.reshape(row_count, -1), value_sum.reshape(row_count, -1)])
            return (jnp.concatenate(query_pieces, axis=0), stacked)

        def skip_tile(unused):
            return (
                jnp.zeros((row_count, kv_heads, group_width, HEAD_SIZE), jnp.float32),
                jnp.zeros((2, row_count, kv_heads * HEAD_SIZE), jnp.float32),
            )

        query_more, key_more = lax.cond(live, compute_tile, skip_tile, 0)
        query_acc = query_acc + query_more
        key_parts.append(key_more)
    returned = jnp.zeros((2, row_count, kv_heads * HEAD_SIZE), jnp.float32)
    for hop_index in range(1, HOPS + 1):
        returned = returned + from_behind(key_parts[hop_index - 1], "blk", -hop_index)
    key_total = (key_gradient_running.reshape(row_count, -1) + returned[0]).astype(jnp.bfloat16)
    value_total = (value_gradient_running.reshape(row_count, -1) + returned[1]).astype(jnp.bfloat16)
    query_total = query_acc.reshape(row_count, -1).astype(jnp.bfloat16)
    query_grad, key_grad, value_grad = (
        lax.all_to_all(query_total, "uly", split_axis=0, concat_axis=1, tiled=True),
        lax.all_to_all(key_total, "uly", split_axis=0, concat_axis=1, tiled=True),
        lax.all_to_all(value_total, "uly", split_axis=0, concat_axis=1, tiled=True),
    )
    return (query_grad, key_grad, value_grad)


def solution(mesh):
    placed = (
        P(("blk", "uly"), None),
        P(("blk", "uly"), None),
        P(("blk", "uly"), None),
        P(("blk", "uly"), None),
        P(("blk", "uly"), None),
        P(("blk", "uly"), None, None),
        P(("blk", "uly")),
    )
    return jax.shard_map(
        per_device,
        mesh=mesh,
        in_specs=placed,
        out_specs=(P(("blk", "uly"), None), P(("blk", "uly"), None), P(("blk", "uly"), None)),
        check_vma=False,
    )
```

profile of v0, /device:TPU:0, one launch (start us, length us, event | category | flops | bytes accessed | tf_op | source)
XLA Modules:
  0.0 147.4 jit_solution(7984379366214825627)
XLA Ops:
  0.7 4.4 %all-to-all-start.2 = ((f32[128,2,16]{0,2,1:T(8,128)}), f32[128,2,16]{0,2,1:T(8,128)S(1)}, u32[]{:S(2)}, u32[]{:S(2)}) async-start(f32[128,2,16]{0,2,1:T(8,128)} %bitcast.239), calls=%async_computation.2 | async-start | bytes 32768 | tf_op jit(solution)/shard_map/all_to_all | solution.py:71
  5.1 1.7 %copy.289 = bf16[16,2,8,512]{3,2,0,1:T(8,128)(2,1)} copy(bf16[16,2,8,512]{3,2,1,0:T(8,128)(2,1)} %bitcast.225) | data formatting | bytes 524288 | tf_op jit(solution)/shard_map/all_to_all | solution.py:67
  6.8 2.1 %all-to-all-done.2 = f32[128,2,16]{0,2,1:T(8,128)S(1)} async-done(((f32[128,2,16]{0,2,1:T(8,128)}), f32[128,2,16]{0,2,1:T(8,128)S(1)}, u32[]{:S(2)}, u32[]{:S(2)}) %all-to-all-start.2) | async-done | bytes 16416 | tf_op jit(solution)/shard_map/all_to_all | solution.py:71
  8.9 3.4 %all-to-all-start = ((bf16[128,2,512]{2,0,1:T(8,128)(2,1)}), bf16[128,2,512]{2,0,1:T(8,128)(2,1)S(1)}, u32[]{:S(2)}, u32[]{:S(2)}) async-start(bf16[128,2,512]{2,0,1:T(8,128)(2,1)} %bitcast.192), calls=%async_computation | async-start | bytes 524288 | tf_op jit(solution)/shard_map/all_to_all | solution.py:67
  12.4 1.7 %copy.288 = bf16[16,2,8,512]{3,2,0,1:T(8,128)(2,1)} copy(bf16[16,2,8,512]{3,2,1,0:T(8,128)(2,1)} %bitcast.226) | data formatting | bytes 524288 | tf_op jit(solution)/shard_map/all_to_all | solution.py:68
  14.1 3.4 %all-to-all-done = bf16[128,2,512]{2,0,1:T(8,128)(2,1)S(1)} async-done(((bf16[128,2,512]{2,0,1:T(8,128)(2,1)}), bf16[128,2,512]{2,0,1:T(8,128)(2,1)S(1)}, u32[]{:S(2)}, u32[]{:S(2)}) %all-to-all-start) | async-done | bytes 262176 | tf_op jit(solution)/shard_map/all_to_all | solution.py:67
  17.5 3.4 %all-to-all-start.3 = ((bf16[128,2,512]{2,0,1:T(8,128)(2,1)}), bf16[128,2,512]{2,0,1:T(8,128)(2,1)S(1)}, u32[]{:S(2)}, u32[]{:S(2)}) async-start(bf16[128,2,512]{2,0,1:T(8,128)(2,1)} %bitcast.191), calls=%async_computation.3 | async-start | bytes 524288 | tf_op jit(solution)/shard_map/all_to_all | solution.py:68
  21.0 5.2 %all-gather = s32[2,1,128]{2,1,0:T(1,128)S(1)} all-gather(s32[1,1,128]{2,1,0:T(1,128)S(1)} %bitcast.245), channel_id=1, replica_groups=mesh['uly'=2,'blk'=16] {'uly'}, dimensions={0}, use_global_device_ids=true | all-gather | bytes 1536 | tf_op jit(solution)/shard_map/all_gather | solution.py:76
  26.2 1.3 collective-permute-start
  27.5 4.5 %collective-permute-start.2 = (s32[256]{0:T(256)S(1)}, s32[256]{0:T(256)S(1)}, u32[]{:S(2)}, u32[]{:S(2)}) collective-permute-start(s32[256]{0:T(256)S(1)} %bitcast.234), channel_id=1, source_target_pairs={{0,2},{1,3},{2,4},{3,5},{4,6},{5,7},{6,8},{7,9},{8,10},{9,11},{10,... | collective-permute-start | bytes 3080 | tf_op jit(solution)/shard_map/ppermute | solution.py:17
  32.8 3.5 %all-to-all-start.4 = ((bf16[128,2,1024]{2,0,1:T(8,128)(2,1)}), bf16[128,2,1024]{2,0,1:T(8,128)(2,1)S(1)}, u32[]{:S(2)}, u32[]{:S(2)}) async-start(bf16[128,2,1024]{2,0,1:T(8,128)(2,1)} %bitcast.189), calls=%async_computation.4 | async-start | bytes 1048576 | tf_op jit(solution)/shard_map/all_to_all | solution.py:66
  42.6 2.7 %all-to-all-done.4 = bf16[128,2,1024]{2,0,1:T(8,128)(2,1)S(1)} async-done(((bf16[128,2,1024]{2,0,1:T(8,128)(2,1)}), bf16[128,2,1024]{2,0,1:T(8,128)(2,1)S(1)}, u32[]{:S(2)}, u32[]{:S(2)}) %all-to-all-start.4) | async-done | bytes 524320 | tf_op jit(solution)/shard_map/all_to_all | solution.py:66
  45.3 3.5 %all-to-all-start.5 = ((bf16[128,2,1024]{2,0,1:T(8,128)(2,1)}), bf16[128,2,1024]{2,0,1:T(8,128)(2,1)S(1)}, u32[]{:S(2)}, u32[]{:S(2)}) async-start(bf16[128,2,1024]{2,0,1:T(8,128)(2,1)} %bitcast.188), calls=%async_computation.5 | async-start | bytes 1048576 | tf_op jit(solution)/shard_map/all_to_all | solution.py:69
  49.9 2.9 %collective-permute-start.1 = (bf16[2,256,512]{1,2,0:T(8,128)(2,1)}, bf16[2,256,512]{1,2,0:T(8,128)(2,1)}, u32[]{:S(2)}, u32[]{:S(2)}) collective-permute-start(bf16[2,256,512]{1,2,0:T(8,128)(2,1)} %pad_maximum_fusion.2), channel_id=1, source_target_pairs={{0,1},{1,2},{2,3},{3,4},{4,5},{5,6},{6,7},{7,8},{8,9},{9,10},{10,1... | collective-permute-start | bytes 1572872 | tf_op jit(solution)/shard_map/ppermute | solution.py:17
  52.9 3.5 %collective-permute-start.3 = (bf16[2,256,512]{1,2,0:T(8,128)(2,1)}, bf16[2,256,512]{1,2,0:T(8,128)(2,1)}, u32[]{:S(2)}, u32[]{:S(2)}) collective-permute-start(bf16[2,256,512]{1,2,0:T(8,128)(2,1)} %pad_maximum_fusion.2), channel_id=1, source_target_pairs={{0,2},{1,3},{2,4},{3,5},{4,6},{5,7},{6,8},{7,9},{8,10},{9,11},{10,... | collective-permute-start | bytes 1572872 | tf_op jit(solution)/shard_map/ppermute | solution.py:17
  57.6 3.5 %all-to-all-start.1 = ((bf16[128,2,1024]{2,0,1:T(8,128)(2,1)}), bf16[128,2,1024]{2,0,1:T(8,128)(2,1)S(1)}, u32[]{:S(2)}, u32[]{:S(2)}) async-start(bf16[128,2,1024]{2,0,1:T(8,128)(2,1)} %bitcast.190), calls=%async_computation.1 | async-start | bytes 1048576 | tf_op jit(solution)/shard_map/all_to_all | solution.py:65
  61.9 8.2 %all-to-all-done.1 = bf16[128,2,1024]{2,0,1:T(8,128)(2,1)S(1)} async-done(((bf16[128,2,1024]{2,0,1:T(8,128)(2,1)}), bf16[128,2,1024]{2,0,1:T(8,128)(2,1)S(1)}, u32[]{:S(2)}, u32[]{:S(2)}) %all-to-all-start.1) | async-done | bytes 524320 | tf_op jit(solution)/shard_map/all_to_all | solution.py:65
  71.4 1.4 fusion.17
  72.9 2.2 %conditional.2 = (f32[256,4,2,128]{3,0,2,1:T(8,128)}, f32[2,256,512]{1,2,0:T(8,128)}) conditional(s32[]{:T(128)} %convert_element_type.56, () %tuple.24, (s32[256]{0:T(256)S(1)}, s32[256]{0:T(256)S(1)}, bf16[2,256,512]{1,2,0:T(8,128)(2,1)}, bf16[256,4,2,128]{3,2,1,0:T(2,128)(2,1)S(1)}, f32[4,2,256,1]{2,1,0,3:T(2,128)S(1)}, ...), branch_computations={%region_3.4_spmd, %region_4.5_spmd} | conditional | flops 675479552 | bytes 33441920 | solution.py:150
  75.0 1.3 collective-permute-start.4
  76.3 2.1 %conditional.3 = (f32[256,4,2,128]{3,0,2,1:T(8,128)}, f32[2,256,512]{1,2,0:T(8,128)}) conditional(s32[]{:T(128)} %convert_element_type.57, () %tuple.26, (s32[256]{0:T(256)S(1)}, s32[256]{0:T(256)S(1)}, bf16[2,256,512]{1,2,0:T(8,128)(2,1)}, bf16[256,4,2,128]{3,2,1,0:T(2,128)(2,1)S(1)}, f32[4,2,256,1]{2,1,0,3:T(2,128)S(1)}, ...), branch_computations={%region_5.6_spmd, %region_6.7_spmd} | conditional | flops 675479552 | bytes 33441920 | solution.py:150
  78.4 1.5 collective-permute-start.5
  79.9 1.6 %fusion.22 = f32[256,4,128]{2,0,1:T(8,128)S(1)} fusion(bf16[4,2,256,256]{2,3,1,0:T(8,128)(2,1)} %fusion.17, bf16[256,4,2,128]{3,2,1,0:T(2,128)(2,1)S(1)} %reshape.108), kind=kOutput, calls=%fused_computation.39 | convolution fusion | flops 134348800 | bytes 2097152 | tf_op jit(solution)/shard_map/hgmn,mhgd->nhd/dot_general | solution.py:50
  82.7 1.3 reshape.113
  86.1 1.7 %add_convert_fusion = bf16[256,4,2,128]{3,0,2,1:T(8,128)(2,1)S(1)} fusion(f32[256,4,2,128]{3,0,2,1:T(8,128)} %get-tuple-element.60, f32[256,4,2,128]{3,0,2,1:T(8,128)S(1)} %fusion.20, f32[256,4,2,128]{3,0,2,1:T(8,128)} %get-tuple-element.59), kind=kLoop, calls=%fused_computation.42 | loop fusion | flops 786432 | bytes 3670016 | tf_op jit(solution)/shard_map/convert_element_type | solution.py:158
  89.6 3.5 %all-to-all-start.6 = ((bf16[2,128,1024]{2,1,0:T(8,128)(2,1)}), bf16[2,128,1024]{2,1,0:T(8,128)(2,1)S(1)}, u32[]{:S(2)}, u32[]{:S(2)}) async-start(bf16[2,128,1024]{2,1,0:T(8,128)(2,1)} %convert_element_type.59), calls=%async_computation.6 | async-start | bytes 1048576 | tf_op jit(solution)/shard_map/all_to_all | solution.py:160
  93.1 32.8 %collective-permute-done.5 = f32[2,256,512]{1,2,0:T(8,128)} collective-permute-done((f32[2,256,512]{1,2,0:T(8,128)}, f32[2,256,512]{1,2,0:T(8,128)}, u32[]{:S(2)}, u32[]{:S(2)}) %collective-permute-start.5) | collective-permute-done | bytes 1048608 | tf_op jit(solution)/shard_map/ppermute | solution.py:17
  125.8 1.7 %add.28 = f32[2,256,512]{1,2,0:T(8,128)S(1)} add(f32[2,256,512]{1,2,0:T(8,128)} %collective-permute-done.4, f32[2,256,512]{1,2,0:T(8,128)} %collective-permute-done.5) | non-fusion elementwise | flops 262144 | bytes 3145728 | tf_op jit(solution)/shard_map/add | solution.py:155
  128.8 3.4 %all-to-all-start.7 = ((bf16[2,128,512]{2,1,0:T(8,128)(2,1)}), bf16[2,128,512]{2,1,0:T(8,128)(2,1)S(1)}, u32[]{:S(2)}, u32[]{:S(2)}) async-start(bf16[2,128,512]{2,1,0:T(8,128)(2,1)} %add_convert_fusion.2), calls=%async_computation.7 | async-start | bytes 524288 | tf_op jit(solution)/shard_map/all_to_all | solution.py:161
  133.0 4.7 %all-to-all-done.7 = bf16[2,128,512]{2,1,0:T(8,128)(2,1)S(1)} async-done(((bf16[2,128,512]{2,1,0:T(8,128)(2,1)}), bf16[2,128,512]{2,1,0:T(8,128)(2,1)S(1)}, u32[]{:S(2)}, u32[]{:S(2)}) %all-to-all-start.7) | async-done | bytes 262176 | tf_op jit(solution)/shard_map/all_to_all | solution.py:161
  137.7 3.4 %all-to-all-start.8 = ((bf16[2,128,512]{2,1,0:T(8,128)(2,1)}), bf16[2,128,512]{2,1,0:T(8,128)(2,1)S(1)}, u32[]{:S(2)}, u32[]{:S(2)}) async-start(bf16[2,128,512]{2,1,0:T(8,128)(2,1)} %add_convert_fusion.1), calls=%async_computation.8 | async-start | bytes 524288 | tf_op jit(solution)/shard_map/all_to_all | solution.py:162
  143.5 2.8 %all-to-all-done.8 = bf16[2,128,512]{2,1,0:T(8,128)(2,1)S(1)} async-done(((bf16[2,128,512]{2,1,0:T(8,128)(2,1)}), bf16[2,128,512]{2,1,0:T(8,128)(2,1)S(1)}, u32[]{:S(2)}, u32[]{:S(2)}) %all-to-all-start.8) | async-done | bytes 262176 | tf_op jit(solution)/shard_map/all_to_all | solution.py:162
  (68 shorter events, 23.4 us)
Async XLA Ops:
  0.6 20.4 %copy-start.13 = (s32[128]{0:T(128)S(1)}, s32[128]{0:T(128)}, u32[]{:S(2)}) copy-start(s32[128]{0:T(128)} %param.17) | copy-start | bytes 1540
  0.6 31.4 %copy-start.10 = (bf16[128,2048]{1,0:T(8,128)(2,1)S(1)}, bf16[128,2048]{1,0:T(8,128)(2,1)}, u32[]{:S(2)}) copy-start(bf16[128,2048]{1,0:T(8,128)(2,1)} %param.15) | copy-start | bytes 1572868
  0.7 8.3 %all-to-all-start.2 = ((f32[128,2,16]{0,2,1:T(8,128)}), f32[128,2,16]{0,2,1:T(8,128)S(1)}, u32[]{:S(2)}, u32[]{:S(2)}) async-start(f32[128,2,16]{0,2,1:T(8,128)} %bitcast.239), calls=%async_computation.2 | async-start | bytes 32768 | tf_op jit(solution)/shard_map/all_to_all | solution.py:71
  5.1 31.9 %copy-start.11 = (bf16[128,2048]{1,0:T(8,128)(2,1)S(1)}, bf16[128,2048]{1,0:T(8,128)(2,1)}, u32[]{:S(2)}) copy-start(bf16[128,2048]{1,0:T(8,128)(2,1)} %param.14) | copy-start | bytes 1572868
  8.9 8.6 %all-to-all-start = ((bf16[128,2,512]{2,0,1:T(8,128)(2,1)}), bf16[128,2,512]{2,0,1:T(8,128)(2,1)S(1)}, u32[]{:S(2)}, u32[]{:S(2)}) async-start(bf16[128,2,512]{2,0,1:T(8,128)(2,1)} %bitcast.192), calls=%async_computation | async-start | bytes 524288 | tf_op jit(solution)/shard_map/all_to_all | solution.py:67
  12.4 25.4 %copy-start.12 = (bf16[128,2048]{1,0:T(8,128)(2,1)S(1)}, bf16[128,2048]{1,0:T(8,128)(2,1)}, u32[]{:S(2)}) copy-start(bf16[128,2048]{1,0:T(8,128)(2,1)} %param.11) | copy-start | bytes 1572868
  17.5 15.3 %all-to-all-start.3 = ((bf16[128,2,512]{2,0,1:T(8,128)(2,1)}), bf16[128,2,512]{2,0,1:T(8,128)(2,1)S(1)}, u32[]{:S(2)}, u32[]{:S(2)}) async-start(bf16[128,2,512]{2,0,1:T(8,128)(2,1)} %bitcast.191), calls=%async_computation.3 | async-start | bytes 524288 | tf_op jit(solution)/shard_map/all_to_all | solution.py:68
  26.2 12.4 %collective-permute-start = (s32[256]{0:T(256)S(1)}, s32[256]{0:T(256)S(1)}, u32[]{:S(2)}, u32[]{:S(2)}) collective-permute-start(s32[256]{0:T(256)S(1)} %bitcast.233), channel_id=1, source_target_pairs={{0,1},{1,2},{2,3},{3,4},{4,5},{5,6},{6,7},{7,8},{8,9},{9,10},{10,1... | collective-permute-start | bytes 3080 | tf_op jit(solution)/shard_map/ppermute | solution.py:17
  27.5 13.0 %collective-permute-start.2 = (s32[256]{0:T(256)S(1)}, s32[256]{0:T(256)S(1)}, u32[]{:S(2)}, u32[]{:S(2)}) collective-permute-start(s32[256]{0:T(256)S(1)} %bitcast.234), channel_id=1, source_target_pairs={{0,2},{1,3},{2,4},{3,5},{4,6},{5,7},{6,8},{7,9},{8,10},{9,11},{10,... | collective-permute-start | bytes 3080 | tf_op jit(solution)/shard_map/ppermute | solution.py:17
  32.8 12.5 %all-to-all-start.4 = ((bf16[128,2,1024]{2,0,1:T(8,128)(2,1)}), bf16[128,2,1024]{2,0,1:T(8,128)(2,1)S(1)}, u32[]{:S(2)}, u32[]{:S(2)}) async-start(bf16[128,2,1024]{2,0,1:T(8,128)(2,1)} %bitcast.189), calls=%async_computation.4 | async-start | bytes 1048576 | tf_op jit(solution)/shard_map/all_to_all | solution.py:66
  45.3 12.3 %all-to-all-start.5 = ((bf16[128,2,1024]{2,0,1:T(8,128)(2,1)}), bf16[128,2,1024]{2,0,1:T(8,128)(2,1)S(1)}, u32[]{:S(2)}, u32[]{:S(2)}) async-start(bf16[128,2,1024]{2,0,1:T(8,128)(2,1)} %bitcast.188), calls=%async_computation.5 | async-start | bytes 1048576 | tf_op jit(solution)/shard_map/all_to_all | solution.py:69
  49.9 22.9 %collective-permute-start.1 = (bf16[2,256,512]{1,2,0:T(8,128)(2,1)}, bf16[2,256,512]{1,2,0:T(8,128)(2,1)}, u32[]{:S(2)}, u32[]{:S(2)}) collective-permute-start(bf16[2,256,512]{1,2,0:T(8,128)(2,1)} %pad_maximum_fusion.2), channel_id=1, source_target_pairs={{0,1},{1,2},{2,3},{3,4},{4,5},{5,6},{6,7},{7,8},{8,9},{9,10},{10,1... | collective-permute-start | bytes 1572872 | tf_op jit(solution)/shard_map/ppermute | solution.py:17
  52.9 23.5 %collective-permute-start.3 = (bf16[2,256,512]{1,2,0:T(8,128)(2,1)}, bf16[2,256,512]{1,2,0:T(8,128)(2,1)}, u32[]{:S(2)}, u32[]{:S(2)}) collective-permute-start(bf16[2,256,512]{1,2,0:T(8,128)(2,1)} %pad_maximum_fusion.2), channel_id=1, source_target_pairs={{0,2},{1,3},{2,4},{3,5},{4,6},{5,7},{6,8},{7,9},{8,10},{9,11},{10,... | collective-permute-start | bytes 1572872 | tf_op jit(solution)/shard_map/ppermute | solution.py:17
  57.6 12.5 %all-to-all-start.1 = ((bf16[128,2,1024]{2,0,1:T(8,128)(2,1)}), bf16[128,2,1024]{2,0,1:T(8,128)(2,1)S(1)}, u32[]{:S(2)}, u32[]{:S(2)}) async-start(bf16[128,2,1024]{2,0,1:T(8,128)(2,1)} %bitcast.190), calls=%async_computation.1 | async-start | bytes 1048576 | tf_op jit(solution)/shard_map/all_to_all | solution.py:65
  70.5 1.0 copy-start.9
  75.0 18.0 %collective-permute-start.4 = (f32[2,256,512]{1,2,0:T(8,128)}, f32[2,256,512]{1,2,0:T(8,128)}, u32[]{:S(2)}, u32[]{:S(2)}) collective-permute-start(f32[2,256,512]{1,2,0:T(8,128)} %get-tuple-element.61), channel_id=1, source_target_pairs={{1,0},{2,1},{3,2},{4,3},{5,4},{6,5},{7,6},{8,7},{9,8},{10,9},{11,1... | collective-permute-start | bytes 3145736 | tf_op jit(solution)/shard_map/ppermute | solution.py:17
  78.4 47.4 %collective-permute-start.5 = (f32[2,256,512]{1,2,0:T(8,128)}, f32[2,256,512]{1,2,0:T(8,128)}, u32[]{:S(2)}, u32[]{:S(2)}) collective-permute-start(f32[2,256,512]{1,2,0:T(8,128)} %get-tuple-element.62), channel_id=1, source_target_pairs={{2,0},{3,1},{4,2},{5,3},{6,4},{7,5},{8,6},{9,7},{10,8},{11,9},{12,... | collective-permute-start | bytes 3145736 | tf_op jit(solution)/shard_map/ppermute | solution.py:17
  84.4 1.2 copy-start.4
  89.6 39.2 %all-to-all-start.6 = ((bf16[2,128,1024]{2,1,0:T(8,128)(2,1)}), bf16[2,128,1024]{2,1,0:T(8,128)(2,1)S(1)}, u32[]{:S(2)}, u32[]{:S(2)}) async-start(bf16[2,128,1024]{2,1,0:T(8,128)(2,1)} %convert_element_type.59), calls=%async_computation.6 | async-start | bytes 1048576 | tf_op jit(solution)/shard_map/all_to_all | solution.py:160
  128.8 8.9 %all-to-all-start.7 = ((bf16[2,128,512]{2,1,0:T(8,128)(2,1)}), bf16[2,128,512]{2,1,0:T(8,128)(2,1)S(1)}, u32[]{:S(2)}, u32[]{:S(2)}) async-start(bf16[2,128,512]{2,1,0:T(8,128)(2,1)} %add_convert_fusion.2), calls=%async_computation.7 | async-start | bytes 524288 | tf_op jit(solution)/shard_map/all_to_all | solution.py:161
  137.7 8.6 %all-to-all-start.8 = ((bf16[2,128,512]{2,1,0:T(8,128)(2,1)}), bf16[2,128,512]{2,1,0:T(8,128)(2,1)S(1)}, u32[]{:S(2)}, u32[]{:S(2)}) async-start(bf16[2,128,512]{2,1,0:T(8,128)(2,1)} %add_convert_fusion.1), calls=%async_computation.8 | async-start | bytes 524288 | tf_op jit(solution)/shard_map/all_to_all | solution.py:162
where the time goes:
time: 149 us; the launch traced here: 147 us
  waiting for transfers between devices  56.8 us (38%)
  starting transfers between devices  47.1 us (32%)
  local copies, waits for them, and re-layouts  23.5 us (16%)
  other arithmetic  6.48 us (4%)
  blocking collectives  5.24 us (4%)
  matrix products  4.65 us (3%)
  between operations  3.64 us (2%)
    ppermute x6, waiting for transfers between devices, from_behind(): return lax.ppermute(block, axis, route)  32.8 us
    ppermute x6, starting transfers between devices, from_behind(): return lax.ppermute(block, axis, route)  14.9 us
    all_to_all x1, waiting for transfers between devices, per_device(): lax.all_to_all(query_inputs, 'uly', split_axis=1, concat_axis=0, tiled=True)  8.18 us
    all_gather x1, blocking collectives, per_device(): ids_loc = lax.all_gather(segment_ids, 'uly', axis=0, tiled=True)  5.24 us
    all_to_all x1, waiting for transfers between devices, per_device(): lax.all_to_all(key_total, 'uly', split_axis=0, concat_axis=1, tiled=True)  4.72 us
    all_to_all x1, starting transfers between devices, per_device(): lax.all_to_all(lse_parts.reshape(tok_local, -1), 'uly', split_axis=1, con...  4.41 us
    another operation x4, local copies, waits for them, and re-layouts  4.25 us
    unnamed x16, local copies, waits for them, and re-layouts  3.91 us
  transfers between devices with their start and end apart: 15, of which 7 were waited for; matrix products, arithmetic and copies ran while one was open for 22% of the time, Pallas kernels for 0%

commit v1 on v0

--- a/solution.py
+++ b/solution.py
@@ -158,7 +158,12 @@
     query_total = query_acc.reshape(row_count, -1).astype(jnp.bfloat16)
     query_grad, key_grad, value_grad = (
         lax.all_to_all(query_total, "uly", split_axis=0, concat_axis=1, tiled=True),
-        lax.all_to_all(key_total, "uly", split_axis=0, concat_axis=1, tiled=True),
+        jnp.concatenate(
+            lax.all_to_all(
+                jnp.stack(jnp.split(key_total, lax.axis_size("uly"), axis=0)), "uly", 0, 0
+            ),
+            axis=1,
+        ),
         lax.all_to_all(value_total, "uly", split_axis=0, concat_axis=1, tiled=True),
     )
     return (query_grad, key_grad, value_grad)

time: 149 us -> 154 us (1.034)
  waiting for transfers between devices: 56.8 us -> 60 us
    ppermute x6, waiting for transfers between devices: 32.8 us -> 35.5 us  [from_behind(): return lax.ppermute(block, axis, route)]
    reshape x1 -> x2, local copies, waits for them, and re-layouts: 0.37 us -> 2.68 us  [per_device(): query_quad = query_loc.reshape(row_count, kv_heads, group_width, HEAD_SIZE)]
    reshape x1, local copies, waits for them, and re-layouts: 0.21 us -> 2.06 us  [per_device(): value_gradient_running.reshape(row_count, -1) + returned[1]]
    unnamed x16 -> x17, local copies, waits for them, and re-layouts: 3.91 us -> 2.1 us
    another operation x4 -> x5, local copies, waits for them, and re-layouts: 4.25 us -> 4.29 us
  transfers between devices with their start and end apart: 15 -> 15, of which waited for: 7 -> 9; matrix products, arithmetic and copies ran while one was open for 22% -> 23% of each run, Pallas kernels for 0% -> 0%
where the time goes in v1:
time: 154 us; the launch traced here: 153 us
  waiting for transfers between devices  60 us (39%)
  starting transfers between devices  47.8 us (31%)
  local copies, waits for them, and re-layouts  24.7 us (16%)
  other arithmetic  6.46 us (4%)
  blocking collectives  5.24 us (3%)
  matrix products  5.24 us (3%)
  between operations  3.64 us (2%)
    ppermute x6, waiting for transfers between devices, from_behind(): return lax.ppermute(block, axis, route)  35.5 us
    ppermute x6, starting transfers between devices, from_behind(): return lax.ppermute(block, axis, route)  15 us
    all_to_all x1, waiting for transfers between devices, per_device(): lax.all_to_all(query_inputs, 'uly', split_axis=1, concat_axis=0, tiled=True)  8.14 us
    all_gather x1, blocking collectives, per_device(): ids_loc = lax.all_gather(segment_ids, 'uly', axis=0, tiled=True)  5.24 us
    all_to_all x1, waiting for transfers between devices, per_device(): lax.all_to_all(jnp.stack(jnp.split(key_total, lax.axis_size('uly'), axis=...  4.77 us
    all_to_all x1, starting transfers between devices, per_device(): lax.all_to_all(lse_parts.reshape(tok_local, -1), 'uly', split_axis=1, con...  4.41 us
    another operation x4, local copies, waits for them, and re-layouts  4.27 us
    all_to_all x1, starting transfers between devices, per_device(): lax.all_to_all(query_inputs, 'uly', split_axis=1, concat_axis=0, tiled=True)  4.2 us
  transfers between devices with their start and end apart: 15, of which 9 were waited for; matrix products, arithmetic and copies ran while one was open for 23% of the time, Pallas kernels for 0%

profile of v1, /device:TPU:0, one launch (start us, length us, event | category | flops | bytes accessed | tf_op | source)
XLA Modules:
  0.0 153.1 jit_solution(10654347679116083511)
XLA Ops:
  0.7 4.4 %all-to-all-start.2 = ((f32[128,2,16]{0,2,1:T(8,128)}), f32[128,2,16]{0,2,1:T(8,128)S(1)}, u32[]{:S(2)}, u32[]{:S(2)}) async-start(f32[128,2,16]{0,2,1:T(8,128)} %bitcast.248), calls=%async_computation.2 | async-start | bytes 32768 | tf_op jit(solution)/shard_map/all_to_all | solution.py:71
  5.1 1.7 %copy.283 = bf16[16,2,8,512]{3,2,0,1:T(8,128)(2,1)} copy(bf16[16,2,8,512]{3,2,1,0:T(8,128)(2,1)} %bitcast.234) | data formatting | bytes 524288 | tf_op jit(solution)/shard_map/all_to_all | solution.py:67
  6.8 2.1 %all-to-all-done.2 = f32[128,2,16]{0,2,1:T(8,128)S(1)} async-done(((f32[128,2,16]{0,2,1:T(8,128)}), f32[128,2,16]{0,2,1:T(8,128)S(1)}, u32[]{:S(2)}, u32[]{:S(2)}) %all-to-all-start.2) | async-done | bytes 16416 | tf_op jit(solution)/shard_map/all_to_all | solution.py:71
  8.9 3.4 %all-to-all-start = ((bf16[128,2,512]{2,0,1:T(8,128)(2,1)}), bf16[128,2,512]{2,0,1:T(8,128)(2,1)S(1)}, u32[]{:S(2)}, u32[]{:S(2)}) async-start(bf16[128,2,512]{2,0,1:T(8,128)(2,1)} %bitcast.204), calls=%async_computation | async-start | bytes 524288 | tf_op jit(solution)/shard_map/all_to_all | solution.py:67
  12.4 1.7 %copy.282 = bf16[16,2,8,512]{3,2,0,1:T(8,128)(2,1)} copy(bf16[16,2,8,512]{3,2,1,0:T(8,128)(2,1)} %bitcast.235) | data formatting | bytes 524288 | tf_op jit(solution)/shard_map/all_to_all | solution.py:68
  14.1 3.4 %all-to-all-done = bf16[128,2,512]{2,0,1:T(8,128)(2,1)S(1)} async-done(((bf16[128,2,512]{2,0,1:T(8,128)(2,1)}), bf16[128,2,512]{2,0,1:T(8,128)(2,1)S(1)}, u32[]{:S(2)}, u32[]{:S(2)}) %all-to-all-start) | async-done | bytes 262176 | tf_op jit(solution)/shard_map/all_to_all | solution.py:67
  17.5 3.4 %all-to-all-start.3 = ((bf16[128,2,512]{2,0,1:T(8,128)(2,1)}), bf16[128,2,512]{2,0,1:T(8,128)(2,1)S(1)}, u32[]{:S(2)}, u32[]{:S(2)}) async-start(bf16[128,2,512]{2,0,1:T(8,128)(2,1)} %bitcast.203), calls=%async_computation.3 | async-start | bytes 524288 | tf_op jit(solution)/shard_map/all_to_all | solution.py:68
  21.0 5.2 %all-gather = s32[2,1,128]{2,1,0:T(1,128)S(1)} all-gather(s32[1,1,128]{2,1,0:T(1,128)S(1)} %bitcast.254), channel_id=1, replica_groups=mesh['uly'=2,'blk'=16] {'uly'}, dimensions={0}, use_global_device_ids=true | all-gather | bytes 1536 | tf_op jit(solution)/shard_map/all_gather | solution.py:76
  27.5 4.5 %collective-permute-start.2 = (s32[256]{0:T(256)S(1)}, s32[256]{0:T(256)S(1)}, u32[]{:S(2)}, u32[]{:S(2)}) collective-permute-start(s32[256]{0:T(256)S(1)} %bitcast.243), channel_id=1, source_target_pairs={{0,2},{1,3},{2,4},{3,5},{4,6},{5,7},{6,8},{7,9},{8,10},{9,11},{10,... | collective-permute-start | bytes 3080 | tf_op jit(solution)/shard_map/ppermute | solution.py:17
  32.8 3.5 %all-to-all-start.4 = ((bf16[128,2,1024]{2,0,1:T(8,128)(2,1)}), bf16[128,2,1024]{2,0,1:T(8,128)(2,1)S(1)}, u32[]{:S(2)}, u32[]{:S(2)}) async-start(bf16[128,2,1024]{2,0,1:T(8,128)(2,1)} %bitcast.201), calls=%async_computation.4 | async-start | bytes 1048576 | tf_op jit(solution)/shard_map/all_to_all | solution.py:66
  42.6 2.7 %all-to-all-done.4 = bf16[128,2,1024]{2,0,1:T(8,128)(2,1)S(1)} async-done(((bf16[128,2,1024]{2,0,1:T(8,128)(2,1)}), bf16[128,2,1024]{2,0,1:T(8,128)(2,1)S(1)}, u32[]{:S(2)}, u32[]{:S(2)}) %all-to-all-start.4) | async-done | bytes 524320 | tf_op jit(solution)/shard_map/all_to_all | solution.py:66
  45.3 3.5 %all-to-all-start.5 = ((bf16[128,2,1024]{2,0,1:T(8,128)(2,1)}), bf16[128,2,1024]{2,0,1:T(8,128)(2,1)S(1)}, u32[]{:S(2)}, u32[]{:S(2)}) async-start(bf16[128,2,1024]{2,0,1:T(8,128)(2,1)} %bitcast.200), calls=%async_computation.5 | async-start | bytes 1048576 | tf_op jit(solution)/shard_map/all_to_all | solution.py:69
  49.9 2.9 %collective-permute-start.1 = (bf16[2,256,512]{1,2,0:T(8,128)(2,1)}, bf16[2,256,512]{1,2,0:T(8,128)(2,1)}, u32[]{:S(2)}, u32[]{:S(2)}) collective-permute-start(bf16[2,256,512]{1,2,0:T(8,128)(2,1)} %pad_maximum_fusion.2), channel_id=1, source_target_pairs={{0,1},{1,2},{2,3},{3,4},{4,5},{5,6},{6,7},{7,8},{8,9},{9,10},{10,1... | collective-permute-start | bytes 1572872 | tf_op jit(solution)/shard_map/ppermute | solution.py:17
  52.9 3.4 %collective-permute-start.3 = (bf16[2,256,512]{1,2,0:T(8,128)(2,1)}, bf16[2,256,512]{1,2,0:T(8,128)(2,1)}, u32[]{:S(2)}, u32[]{:S(2)}) collective-permute-start(bf16[2,256,512]{1,2,0:T(8,128)(2,1)} %pad_maximum_fusion.2), channel_id=1, source_target_pairs={{0,2},{1,3},{2,4},{3,5},{4,6},{5,7},{6,8},{7,9},{8,10},{9,11},{10,... | collective-permute-start | bytes 1572872 | tf_op jit(solution)/shard_map/ppermute | solution.py:17
  57.4 4.2 %all-to-all-start.1 = ((bf16[128,2,1024]{2,0,1:T(8,128)(2,1)}), bf16[128,2,1024]{2,0,1:T(8,128)(2,1)}, u32[]{:S(2)}, u32[]{:S(2)}) async-start(bf16[128,2,1024]{2,0,1:T(8,128)(2,1)} %bitcast.202), calls=%async_computation.1 | async-start | bytes 1048576 | tf_op jit(solution)/shard_map/all_to_all | solution.py:65
  62.8 8.1 %all-to-all-done.1 = bf16[128,2,1024]{2,0,1:T(8,128)(2,1)} async-done(((bf16[128,2,1024]{2,0,1:T(8,128)(2,1)}), bf16[128,2,1024]{2,0,1:T(8,128)(2,1)}, u32[]{:S(2)}, u32[]{:S(2)}) %all-to-all-start.1) | async-done | bytes 524320 | tf_op jit(solution)/shard_map/all_to_all | solution.py:65
  71.0 1.4 reshape.109
  73.6 1.6 %fusion.19 = f32[4,2,256,256]{2,3,1,0:T(8,128)S(1)} fusion(bf16[256,4,2,128]{0,3,2,1:T(8,128)(2,1)} %copy.202, f32[4,2,256]{2,1,0:T(2,128)S(1)} %bitcast.249, pred[256,256]{0,1:T(8,128)(4,1)S(1)} %fusion.28, bf16[256,4,128,1]{2,1,0,3:T(4,128)(2,1)S(1)} %bitcast.219), kind=kOutput, calls=%fused_computation.33 | convolution fusion | flops 135790592 | bytes 2957312 | tf_op jit(solution)/shard_map/mhgd,nhd->hgmn/dot_general | solution.py:34
  76.8 2.1 %reshape.117 = f32[2,128,512]{2,1,0:T(8,128)} reshape(f32[256,4,128]{2,1,0:T(4,128)} %copy.205) | data formatting | bytes 1048576 | tf_op jit(solution)/shard_map/reshape | solution.py:157
  78.9 2.2 %conditional.2 = (f32[256,4,2,128]{3,0,2,1:T(8,128)}, f32[2,256,512]{1,2,0:T(8,128)}) conditional(s32[]{:T(128)} %convert_element_type.55, () %tuple.24, (s32[256]{0:T(256)S(1)}, s32[256]{0:T(256)S(1)}, bf16[2,256,512]{1,2,0:T(8,128)(2,1)}, bf16[256,4,2,128]{3,2,1,0:T(2,128)(2,1)S(1)}, f32[4,2,256,1]{2,1,0,3:T(2,128)S(1)}, ...), branch_computations={%region_3.4_spmd, %region_4.5_spmd} | conditional | flops 675479552 | bytes 33441920 | solution.py:150
  81.1 1.3 collective-permute-start.4
  82.4 2.1 %conditional.3 = (f32[256,4,2,128]{3,0,2,1:T(8,128)}, f32[2,256,512]{1,2,0:T(8,128)}) conditional(s32[]{:T(128)} %convert_element_type.56, () %tuple.26, (s32[256]{0:T(256)S(1)}, s32[256]{0:T(256)S(1)}, bf16[2,256,512]{1,2,0:T(8,128)(2,1)}, bf16[256,4,2,128]{3,2,1,0:T(2,128)(2,1)S(1)}, f32[4,2,256,1]{2,1,0,3:T(2,128)S(1)}, ...), branch_computations={%region_5.6_spmd, %region_6.7_spmd} | conditional | flops 675479552 | bytes 31344740 | solution.py:150
  84.5 1.6 %collective-permute-start.5 = (f32[2,256,512]{1,2,0:T(8,128)}, f32[2,256,512]{1,2,0:T(8,128)}, u32[]{:S(2)}, u32[]{:S(2)}) collective-permute-start(f32[2,256,512]{1,2,0:T(8,128)} %get-tuple-element.62), channel_id=1, source_target_pairs={{2,0},{3,1},{4,2},{5,3},{6,4},{7,5},{8,6},{9,7},{10,8},{11,9},{12,... | collective-permute-start | bytes 3145736 | tf_op jit(solution)/shard_map/ppermute | solution.py:17
  86.1 1.4 fusion.17
  89.3 1.7 %add_convert_fusion = bf16[256,4,2,128]{3,0,2,1:T(8,128)(2,1)S(1)} fusion(f32[256,4,2,128]{3,0,2,1:T(8,128)} %get-tuple-element.60, f32[256,4,2,128]{3,0,2,1:T(8,128)S(1)} %fusion.20, f32[256,4,2,128]{3,0,2,1:T(8,128)} %get-tuple-element.59), kind=kLoop, calls=%fused_computation.41 | loop fusion | flops 786432 | bytes 3670016 | tf_op jit(solution)/shard_map/convert_element_type | solution.py:158
  92.7 3.5 %all-to-all-start.6 = ((bf16[2,128,1024]{2,1,0:T(8,128)(2,1)}), bf16[2,128,1024]{2,1,0:T(8,128)(2,1)S(1)}, u32[]{:S(2)}, u32[]{:S(2)}) async-start(bf16[2,128,1024]{2,1,0:T(8,128)(2,1)} %convert_element_type.58), calls=%async_computation.6 | async-start | bytes 1048576 | tf_op jit(solution)/shard_map/all_to_all | solution.py:160
  97.0 34.7 %collective-permute-done.5 = f32[2,256,512]{1,2,0:T(8,128)} collective-permute-done((f32[2,256,512]{1,2,0:T(8,128)}, f32[2,256,512]{1,2,0:T(8,128)}, u32[]{:S(2)}, u32[]{:S(2)}) %collective-permute-start.5) | collective-permute-done | bytes 1048608 | tf_op jit(solution)/shard_map/ppermute | solution.py:17
  131.7 1.7 %add.27 = f32[2,256,512]{1,2,0:T(8,128)S(1)} add(f32[2,256,512]{1,2,0:T(8,128)} %collective-permute-done.4, f32[2,256,512]{1,2,0:T(8,128)} %collective-permute-done.5) | non-fusion elementwise | flops 262144 | bytes 3145728 | tf_op jit(solution)/shard_map/add | solution.py:155
  134.5 3.4 %all-to-all-start.7 = ((bf16[2,128,512]{1,2,0:T(8,128)(2,1)}), bf16[2,128,512]{1,2,0:T(8,128)(2,1)S(1)}, u32[]{:S(2)}, u32[]{:S(2)}) async-start(bf16[2,128,512]{1,2,0:T(8,128)(2,1)} %pad_maximum_fusion.3), calls=%async_computation.7 | async-start | bytes 524288 | tf_op jit(solution)/shard_map/all_to_all | solution.py:162
  138.7 4.8 %all-to-all-done.7 = bf16[2,128,512]{1,2,0:T(8,128)(2,1)S(1)} async-done(((bf16[2,128,512]{1,2,0:T(8,128)(2,1)}), bf16[2,128,512]{1,2,0:T(8,128)(2,1)S(1)}, u32[]{:S(2)}, u32[]{:S(2)}) %all-to-all-start.7) | async-done | bytes 262176 | tf_op jit(solution)/shard_map/all_to_all | solution.py:162
  143.5 3.4 %all-to-all-start.8 = ((bf16[2,128,512]{2,1,0:T(8,128)(2,1)}), bf16[2,128,512]{2,1,0:T(8,128)(2,1)S(1)}, u32[]{:S(2)}, u32[]{:S(2)}) async-start(bf16[2,128,512]{2,1,0:T(8,128)(2,1)} %add_convert_fusion.1), calls=%async_computation.8 | async-start | bytes 524288 | tf_op jit(solution)/shard_map/all_to_all | solution.py:167
  149.1 3.0 %all-to-all-done.8 = bf16[2,128,512]{2,1,0:T(8,128)(2,1)S(1)} async-done(((bf16[2,128,512]{2,1,0:T(8,128)(2,1)}), bf16[2,128,512]{2,1,0:T(8,128)(2,1)S(1)}, u32[]{:S(2)}, u32[]{:S(2)}) %all-to-all-start.8) | async-done | bytes 262176 | tf_op jit(solution)/shard_map/all_to_all | solution.py:167
  (69 shorter events, 25.4 us)
Async XLA Ops:
  0.6 20.4 %copy-start.13 = (s32[128]{0:T(128)S(1)}, s32[128]{0:T(128)}, u32[]{:S(2)}) copy-start(s32[128]{0:T(128)} %param.17) | copy-start | bytes 1540
  0.6 31.4 %copy-start.10 = (bf16[128,2048]{1,0:T(8,128)(2,1)S(1)}, bf16[128,2048]{1,0:T(8,128)(2,1)}, u32[]{:S(2)}) copy-start(bf16[128,2048]{1,0:T(8,128)(2,1)} %param.15) | copy-start | bytes 1572868
  0.7 8.3 %all-to-all-start.2 = ((f32[128,2,16]{0,2,1:T(8,128)}), f32[128,2,16]{0,2,1:T(8,128)S(1)}, u32[]{:S(2)}, u32[]{:S(2)}) async-start(f32[128,2,16]{0,2,1:T(8,128)} %bitcast.248), calls=%async_computation.2 | async-start | bytes 32768 | tf_op jit(solution)/shard_map/all_to_all | solution.py:71
  5.1 31.9 %copy-start.11 = (bf16[128,2048]{1,0:T(8,128)(2,1)S(1)}, bf16[128,2048]{1,0:T(8,128)(2,1)}, u32[]{:S(2)}) copy-start(bf16[128,2048]{1,0:T(8,128)(2,1)} %param.14) | copy-start | bytes 1572868
  8.9 8.6 %all-to-all-start = ((bf16[128,2,512]{2,0,1:T(8,128)(2,1)}), bf16[128,2,512]{2,0,1:T(8,128)(2,1)S(1)}, u32[]{:S(2)}, u32[]{:S(2)}) async-start(bf16[128,2,512]{2,0,1:T(8,128)(2,1)} %bitcast.204), calls=%async_computation | async-start | bytes 524288 | tf_op jit(solution)/shard_map/all_to_all | solution.py:67
  12.4 25.4 %copy-start.12 = (bf16[128,2048]{1,0:T(8,128)(2,1)S(1)}, bf16[128,2048]{1,0:T(8,128)(2,1)}, u32[]{:S(2)}) copy-start(bf16[128,2048]{1,0:T(8,128)(2,1)} %param.11) | copy-start | bytes 1572868
  17.5 15.3 %all-to-all-start.3 = ((bf16[128,2,512]{2,0,1:T(8,128)(2,1)}), bf16[128,2,512]{2,0,1:T(8,128)(2,1)S(1)}, u32[]{:S(2)}, u32[]{:S(2)}) async-start(bf16[128,2,512]{2,0,1:T(8,128)(2,1)} %bitcast.203), calls=%async_computation.3 | async-start | bytes 524288 | tf_op jit(solution)/shard_map/all_to_all | solution.py:68
  26.2 12.4 %collective-permute-start = (s32[256]{0:T(256)S(1)}, s32[256]{0:T(256)S(1)}, u32[]{:S(2)}, u32[]{:S(2)}) collective-permute-start(s32[256]{0:T(256)S(1)} %bitcast.242), channel_id=1, source_target_pairs={{0,1},{1,2},{2,3},{3,4},{4,5},{5,6},{6,7},{7,8},{8,9},{9,10},{10,1... | collective-permute-start | bytes 3080 | tf_op jit(solution)/shard_map/ppermute | solution.py:17
  27.5 13.0 %collective-permute-start.2 = (s32[256]{0:T(256)S(1)}, s32[256]{0:T(256)S(1)}, u32[]{:S(2)}, u32[]{:S(2)}) collective-permute-start(s32[256]{0:T(256)S(1)} %bitcast.243), channel_id=1, source_target_pairs={{0,2},{1,3},{2,4},{3,5},{4,6},{5,7},{6,8},{7,9},{8,10},{9,11},{10,... | collective-permute-start | bytes 3080 | tf_op jit(solution)/shard_map/ppermute | solution.py:17
  32.8 12.5 %all-to-all-start.4 = ((bf16[128,2,1024]{2,0,1:T(8,128)(2,1)}), bf16[128,2,1024]{2,0,1:T(8,128)(2,1)S(1)}, u32[]{:S(2)}, u32[]{:S(2)}) async-start(bf16[128,2,1024]{2,0,1:T(8,128)(2,1)} %bitcast.201), calls=%async_computation.4 | async-start | bytes 1048576 | tf_op jit(solution)/shard_map/all_to_all | solution.py:66
  45.3 12.1 %all-to-all-start.5 = ((bf16[128,2,1024]{2,0,1:T(8,128)(2,1)}), bf16[128,2,1024]{2,0,1:T(8,128)(2,1)S(1)}, u32[]{:S(2)}, u32[]{:S(2)}) async-start(bf16[128,2,1024]{2,0,1:T(8,128)(2,1)} %bitcast.200), calls=%async_computation.5 | async-start | bytes 1048576 | tf_op jit(solution)/shard_map/all_to_all | solution.py:69
  49.9 29.0 %collective-permute-start.1 = (bf16[2,256,512]{1,2,0:T(8,128)(2,1)}, bf16[2,256,512]{1,2,0:T(8,128)(2,1)}, u32[]{:S(2)}, u32[]{:S(2)}) collective-permute-start(bf16[2,256,512]{1,2,0:T(8,128)(2,1)} %pad_maximum_fusion.2), channel_id=1, source_target_pairs={{0,1},{1,2},{2,3},{3,4},{4,5},{5,6},{6,7},{7,8},{8,9},{9,10},{10,1... | collective-permute-start | bytes 1572872 | tf_op jit(solution)/shard_map/ppermute | solution.py:17
  52.9 29.5 %collective-permute-start.3 = (bf16[2,256,512]{1,2,0:T(8,128)(2,1)}, bf16[2,256,512]{1,2,0:T(8,128)(2,1)}, u32[]{:S(2)}, u32[]{:S(2)}) collective-permute-start(bf16[2,256,512]{1,2,0:T(8,128)(2,1)} %pad_maximum_fusion.2), channel_id=1, source_target_pairs={{0,2},{1,3},{2,4},{3,5},{4,6},{5,7},{6,8},{7,9},{8,10},{9,11},{10,... | collective-permute-start | bytes 1572872 | tf_op jit(solution)/shard_map/ppermute | solution.py:17
  57.4 13.5 %all-to-all-start.1 = ((bf16[128,2,1024]{2,0,1:T(8,128)(2,1)}), bf16[128,2,1024]{2,0,1:T(8,128)(2,1)}, u32[]{:S(2)}, u32[]{:S(2)}) async-start(bf16[128,2,1024]{2,0,1:T(8,128)(2,1)} %bitcast.202), calls=%async_computation.1 | async-start | bytes 1048576 | tf_op jit(solution)/shard_map/all_to_all | solution.py:65
  81.1 16.0 %collective-permute-start.4 = (f32[2,256,512]{1,2,0:T(8,128)}, f32[2,256,512]{1,2,0:T(8,128)}, u32[]{:S(2)}, u32[]{:S(2)}) collective-permute-start(f32[2,256,512]{1,2,0:T(8,128)} %get-tuple-element.61), channel_id=1, source_target_pairs={{1,0},{2,1},{3,2},{4,3},{5,4},{6,5},{7,6},{8,7},{9,8},{10,9},{11,1... | collective-permute-start | bytes 3145736 | tf_op jit(solution)/shard_map/ppermute | solution.py:17
  84.5 3.0 %copy-start.4 = (bf16[256,4,2,128]{0,3,2,1:T(8,128)(2,1)S(1)}, bf16[256,4,2,128]{0,3,2,1:T(8,128)(2,1)}, u32[]{:S(2)}) copy-start(bf16[256,4,2,128]{0,3,2,1:T(8,128)(2,1)} %copy.202) | copy-start | bytes 1572868
  84.5 47.2 %collective-permute-start.5 = (f32[2,256,512]{1,2,0:T(8,128)}, f32[2,256,512]{1,2,0:T(8,128)}, u32[]{:S(2)}, u32[]{:S(2)}) collective-permute-start(f32[2,256,512]{1,2,0:T(8,128)} %get-tuple-element.62), channel_id=1, source_target_pairs={{2,0},{3,1},{4,2},{5,3},{6,4},{7,5},{8,6},{9,7},{10,8},{11,9},{12,... | collective-permute-start | bytes 3145736 | tf_op jit(solution)/shard_map/ppermute | solution.py:17
  92.7 41.8 %all-to-all-start.6 = ((bf16[2,128,1024]{2,1,0:T(8,128)(2,1)}), bf16[2,128,1024]{2,1,0:T(8,128)(2,1)S(1)}, u32[]{:S(2)}, u32[]{:S(2)}) async-start(bf16[2,128,1024]{2,1,0:T(8,128)(2,1)} %convert_element_type.58), calls=%async_computation.6 | async-start | bytes 1048576 | tf_op jit(solution)/shard_map/all_to_all | solution.py:160
  96.2 37.2 %copy-start.5 = (f32[4,256,128]{1,2,0:T(8,128)S(1)}, f32[4,256,128]{1,2,0:T(8,128)}, u32[]{:S(2)}) copy-start(f32[4,256,128]{1,2,0:T(8,128)} %fusion.21) | copy-start | bytes 1572868
  133.4 4.5 %copy-start.3 = (f32[2,128,512]{2,1,0:T(8,128)S(1)}, f32[2,128,512]{2,1,0:T(8,128)}, u32[]{:S(2)}) copy-start(f32[2,128,512]{2,1,0:T(8,128)} %reshape.117) | copy-start | bytes 1572868
  134.5 9.0 %all-to-all-start.7 = ((bf16[2,128,512]{1,2,0:T(8,128)(2,1)}), bf16[2,128,512]{1,2,0:T(8,128)(2,1)S(1)}, u32[]{:S(2)}, u32[]{:S(2)}) async-start(bf16[2,128,512]{1,2,0:T(8,128)(2,1)} %pad_maximum_fusion.3), calls=%async_computation.7 | async-start | bytes 524288 | tf_op jit(solution)/shard_map/all_to_all | solution.py:162
  143.5 8.6 %all-to-all-start.8 = ((bf16[2,128,512]{2,1,0:T(8,128)(2,1)}), bf16[2,128,512]{2,1,0:T(8,128)(2,1)S(1)}, u32[]{:S(2)}, u32[]{:S(2)}) async-start(bf16[2,128,512]{2,1,0:T(8,128)(2,1)} %add_convert_fusion.1), calls=%async_computation.8 | async-start | bytes 524288 | tf_op jit(solution)/shard_map/all_to_all | solution.py:167
